TPU v7x, 32 devices: a whole 2x2x4 slice. The times are simulated.
32 devices in a mesh: gx: 8 (over y, x, core), gy: 4 (over z).
Axes of the slice: x: 2, y: 2, z: 4, core: 2. Of those that a mesh axis runs over, the one named last changes fastest.
Arguments:
- flow_field: bfloat16 [4, 64, 1024, 512], P(None, None, ('gx', 'gy')), may hold values from -6 to 6
- cotangent: bfloat16 [4, 64, 1024, 512], P(None, None, ('gx', 'gy')), may hold values from -2 to 2
- spectral_weight: bfloat16 [128, 64, 64, 128], P(('gx', 'gy')), may hold values from -0.75 to 0.75
- local_weight: bfloat16 [64, 64], replicated, may hold values from -0.75 to 0.75
- channel_bias: float32 [64], replicated, may hold values from -3 to 3
Outputs:
- output_field: bfloat16 [4, 64, 1024, 512], P(None, None, ('gx', 'gy'))
- grad_field: bfloat16 [4, 64, 1024, 512], P(None, None, ('gx', 'gy'))
- grad_spectral: float32 [128, 64, 64, 128], P(('gx', 'gy'))
All inputs are finite; a program needn't handle non-finite values.
Results may differ from a plain program's by a relative error of at most 0.014.
Values may be sent and summed in bfloat16 or wider, within the bound.
A program may use at most 128 MiB of HBM per device.

v0:
```python
import functools
import math

import jax
import jax.numpy as jnp
import numpy as np
from jax import lax
from jax.experimental import pallas as pl
from jax.experimental.pallas import tpu as pltpu
from jax.sharding import PartitionSpec as P

root_half = 0.7071067811865476
density_norm = 0.3989422804014327
LANES = 128
PACK = 16
MESH = pl.DeviceIdType.MESH
f32, bf16 = jnp.float32, jnp.bfloat16


def basis_table(cells, cols, factor):
    kept = cols // 2
    columns = np.arange(cols)
    frequency = np.where(columns < kept, columns, columns - kept + 1)
    phases = np.arange(cells)[:, None] * frequency[None, :] % cells
    angles = phases.astype(np.float32) * np.float32(2.0 * math.pi / cells)
    values = np.where(columns[None, :] < kept, np.cos(angles), np.sin(angles))
    return jnp.asarray((values * np.float32(factor)).astype(jnp.bfloat16))


def gelu_slope(values):
    cumulative = 0.5 * (1.0 + lax.erf(values * root_half))
    density = jnp.exp(-0.5 * values * values) * density_norm
    return cumulative + values * density


def dot_t(a, b, da, db):
    return lax.dot_general(a, b, (((da,), (db,)), ((), ())), preferred_element_type=f32)


def to_owners(modal_rows):
    return lax.all_to_all(modal_rows, ("gx", "gy"), split_axis=0, concat_axis=1, tiled=True)


def to_slabs(modal_part):
    return lax.all_to_all(modal_part, ("gx", "gy"), split_axis=1, concat_axis=0, tiled=True)


def contract(spec, left, right):
    return jnp.einsum(spec, left, right, preferred_element_type=jnp.float32)


def plain_shards(flow_field, cotangent, spectral_weight, local_weight, channel_bias):
    devices = lax.axis_size("gx") * lax.axis_size("gy")
    planes, channels, slab_rows, cells_along = flow_field.shape
    cells_across = slab_rows * devices
    own_cols = spectral_weight.shape[0]
    mode_cols = spectral_weight.shape[3]
    kept_modes = mode_cols // 2
    both = planes * channels
    scale_inv = math.sqrt(1.0 / kept_modes)
    fwd_x = basis_table(cells_across, mode_cols, math.sqrt(2.0 / cells_across))
    fwd_y = basis_table(cells_along, mode_cols, math.sqrt(2.0 / cells_along))
    inv_x = basis_table(cells_across, mode_cols, scale_inv)
    inv_y = basis_table(cells_along, mode_cols, scale_inv)

    def to_modes(field, table_x, table_y):
        rows = contract("axy,yj->jxa", field.reshape(both, slab_rows, cells_along), table_y)
        received = to_owners(rows.astype(jnp.bfloat16))
        modes = contract("jxa,xk->jka", received, table_x).astype(jnp.bfloat16)
        return modes.reshape(own_cols, mode_cols, planes, channels)

    def to_rows(modes, table_x):
        merged = modes.reshape(own_cols, mode_cols, both)
        return to_slabs(contract("jka,xk->jxa", merged, table_x).astype(jnp.bfloat16))

    def to_space(rows, table_y):
        field = contract("jxa,yj->axy", rows, table_y)
        return field.reshape(planes, channels, slab_rows, cells_along)

    coeffs = to_modes(flow_field, fwd_x, fwd_y)
    mixed = contract("jkzi,jiok->jkzo", coeffs, spectral_weight).astype(jnp.bfloat16)
    gathered = to_rows(mixed, inv_x)
    spectral = to_space(gathered, inv_y)
    pointwise = contract("zixy,io->zoxy", flow_field, local_weight)
    pre_activation = spectral + pointwise + channel_bias[None, :, None, None]
    output_field = jax.nn.gelu(pre_activation, approximate=False).astype(jnp.bfloat16)
    grad_pre = (cotangent.astype(jnp.float32) * gelu_slope(pre_activation)).astype(jnp.bfloat16)
    grad_mixed = to_modes(grad_pre, inv_x, inv_y)
    grad_coeffs = contract("jkzo,jiok->jkzi", grad_mixed, spectral_weight).astype(jnp.bfloat16)
    gathered_back = to_rows(grad_coeffs, fwd_x)
    grad_spectral = contract("jkzi,jkzo->jiok", coeffs, grad_mixed)
    backward = to_space(gathered_back, fwd_y)
    through_local = contract("zoxy,io->zixy", grad_pre, local_weight)
    grad_field = (backward + through_local).astype(jnp.bfloat16)
    return (output_field, grad_field, grad_spectral)


def main_kernel(
    nx, ny, planes, chans, slab, modes, own,
    flow_hbm, cot_hbm, w_hbm, lw_ref, bias_ref, fy_ref, iy_ref, fx_ref, ix_ref,
    out_hbm, gp_hbm, back_hbm, kron_hbm, co_ref, gm_ref,
    fbuf, cbuf, wbuf, tx, kron, kron_t, sbuf, rbuf, part, zs, zr, cf, gf, ms, zg, tg, lhs2, isb,
    gbuf, gt, pre, xs,
    load_sem, cot_sem, store_sem, w_sem, kron_sem, own_sem, s1, r1, s2, r2, s3, r3, s4, r4,
):
    gx, gy = lax.axis_index("gx"), lax.axis_index("gy")
    per = LANES // slab
    groups = chans // per
    jg = modes // nx
    cells = fbuf.shape[3]
    halves = slab // PACK
    width = 2 * LANES
    parts = cells // width

    def load(p):
        return pltpu.make_async_copy(flow_hbm.at[p], fbuf.at[p], load_sem.at[p])

    def load_cot(p):
        return pltpu.make_async_copy(cot_hbm.at[p], cbuf.at[p], cot_sem.at[p])

    def store_out(p):
        return pltpu.make_async_copy(cbuf.at[p], out_hbm.at[p], store_sem.at[0, p])

    def store_gp(p):
        return pltpu.make_async_copy(fbuf.at[p], gp_hbm.at[p], store_sem.at[1, p])

    def load_w():
        return pltpu.make_async_copy(w_hbm, wbuf, w_sem)

    def store_kron():
        return pltpu.make_async_copy(kron_t, kron_hbm, kron_sem)

    for p in range(planes):
        load(p).start()
    load_w().start()
    for p in range(planes):
        load_cot(p).start()

    barrier = pltpu.get_barrier_semaphore()
    for o in range(1, nx):
        pl.semaphore_signal(barrier, inc=1, device_id=((gx + o) % nx, gy), device_id_type=MESH)
    for o in range(1, ny):
        pl.semaphore_signal(barrier, inc=1, device_id=(gx, (gy + o) % ny), device_id_type=MESH)

    def lane(g):
        return pl.ds(pl.multiple_of(g * LANES, LANES), LANES)

    def jrows(g):
        return pl.ds(pl.multiple_of(g * jg, jg), jg)

    def rows(f, p, o, out):
        other = (gx + o) % nx if out else (gx + nx - o) % nx
        slot = gx if out else other
        return pltpu.make_async_remote_copy(
            sbuf.at[f, p, other], rbuf.at[f, p, :, :, lane(slot)], s1.at[f, p, o], r1.at[f, p, o],
            device_id=(other, gy), device_id_type=MESH)

    def sums(f, p, o, out):
        other = (gy + o) % ny if out else (gy + ny - o) % ny
        slot = gy if out else other
        return pltpu.make_async_remote_copy(
            zs.at[f, p, other], zr.at[f, p, slot], s2.at[f, p, o], r2.at[f, p, o],
            device_id=(gx, other), device_id_type=MESH)

    def mixed(f, p, o, out):
        other = (gy + o) % ny if out else (gy + ny - o) % ny
        slot = gy if out else other
        return pltpu.make_async_remote_copy(
            ms.at[f, p], zg.at[f, p, slot], s3.at[f, p, o], r3.at[f, p, o],
            device_id=(gx, other), device_id_type=MESH)

    def back(f, p, o, out):
        other = (gx + o) % nx if out else (gx + nx - o) % nx
        slot = gx if out else other
        into = back_hbm if f else gbuf
        return pltpu.make_async_remote_copy(
            isb.at[f, p, other], into.at[p, :, jrows(slot), :], s4.at[f, p, o], r4.at[f, p, o],
            device_id=(other, gy), device_id_type=MESH)

    def back_own(p):
        return pltpu.make_async_copy(isb.at[1, p, gx], back_hbm.at[p, :, jrows(gx), :], own_sem.at[p])

    def analyse(f, p):
        table = iy_ref if f else fy_ref

        def body(t, carry):
            x = fbuf[p, pl.ds(t * 2 * per, 2 * per)].reshape(2 * LANES, cells)
            r = dot_t(table[...], x, 1, 1).astype(bf16)
            for h in range(2):
                sbuf[f, p, :, t * 2 + h] = r[:, h * LANES:(h + 1) * LANES].reshape(nx, jg, LANES)
            return carry

        lax.fori_loop(0, groups // 2, body, 0, unroll=2)
        rbuf[f, p, :, :, lane(gx)] = sbuf[f, p, gx]

    def send_rows(f, p):
        for o in range(1, nx):
            rows(f, p, o, True).start()

    def across(f, p):
        for o in range(1, nx):
            rows(f, p, o, False).wait_recv()
        left = rbuf[f, p].reshape(groups * jg, nx * LANES)
        r = jnp.dot(left, tx[f], preferred_element_type=f32)
        for g in range(groups):
            for c in range(per):
                part[pl.ds((g * per + c) * jg, jg), :] = r[g * jg:(g + 1) * jg, c * modes:(c + 1) * modes]
        for j in range(jg):
            zs[f, p, j // own, j % own] = part[pl.ds(j, chans, stride=jg), :].astype(bf16)
        zr[f, p, gy] = zs[f, p, gy]
        for o in range(1, ny):
            sums(f, p, o, True).start()

    def mix(f, p):
        for o in range(1, ny):
            sums(f, p, o, False).wait_recv()
        total = zr[f, p, 0].astype(f32)
        for s in range(1, ny):
            total = total + zr[f, p, s].astype(f32)
        coef = total.astype(bf16)
        if f:
            gm_ref[p] = coef
        else:
            co_ref[p] = coef
        cf[...] = coef.astype(f32).reshape(own * chans, modes)
        for j in range(own):
            if f:
                right = cf[pl.ds(j * chans, chans), :]

                def body(i, carry):
                    prod = wbuf[j, i].astype(f32) * right
                    gf[pl.ds(i, 1), :] = jnp.sum(prod, axis=0, keepdims=True)
                    return carry

                lax.fori_loop(0, chans, body, 0, unroll=8)
                ms[f, p, j] = gf[...].astype(bf16)
            else:

                def body(i, acc):
                    return acc + cf[pl.ds(j * chans + i, 1), :] * wbuf[j, i].astype(f32)

                acc = lax.fori_loop(0, chans, body, jnp.zeros((chans, modes), f32), unroll=8)
                ms[f, p, j] = acc.astype(bf16)
        zg[f, p, gy] = ms[f, p]
        for o in range(1, ny):
            mixed(f, p, o, True).start()

    def expand(f, p):
        for o in range(1, ny):
            mixed(f, p, o, False).wait_recv()
        tg[...] = zg[f, p].astype(f32).reshape(ny * own * chans, modes)
        for c in range(chans):
            lhs2[pl.ds((c // per) * jg, jg), pl.ds((c % per) * modes, modes)] = tg[pl.ds(c, jg, stride=chans), :].astype(bf16)

        def body(t, carry):
            table = tx[1 - f, pl.ds(pl.multiple_of(t * 2 * LANES, LANES), 2 * LANES), :]
            r = dot_t(lhs2[...], table, 1, 1).astype(bf16)
            for h in range(2):
                isb[f, p, t * 2 + h] = r[:, h * LANES:(h + 1) * LANES].reshape(groups, jg, LANES)
            return carry

        lax.fori_loop(0, nx // 2, body, 0, unroll=2)
        if f:
            back_own(p).start()
        else:
            gbuf[p, :, jrows(gx), :] = isb[f, p, gx]
        for o in range(1, nx):
            back(f, p, o, True).start()

    def point(p):
        load_cot(p).wait()
        for o in range(1, nx):
            back(0, p, o, False).wait_recv()

        def turn(g, carry):
            block = gbuf[p, g].T.reshape(per, halves, PACK, modes)
            for h in range(halves):
                gt[h, pl.ds(g * per * PACK, per * PACK), :] = block[:, h].reshape(per * PACK, modes)
            return carry

        lax.fori_loop(0, groups, turn, 0, unroll=4)

        def piece(s, carry):
            h, y = s // parts, s % parts
            rows16 = pl.ds(pl.multiple_of(h * PACK, PACK), PACK)
            cols = pl.ds(pl.multiple_of(y * width, width), width)
            xs[...] = fbuf[p, :, rows16, cols].reshape(chans * PACK, width)
            r = jnp.dot(kron[...], xs[...], preferred_element_type=f32)
            r = r + jnp.dot(gt[h], iy_ref[:, cols], preferred_element_type=f32)
            pre[...] = r.reshape(chans, PACK, width)

            def one(c, inner):
                v = pre[c] + bias_ref[c]
                phi = 0.5 + 0.5 * lax.erf(v * root_half)
                density = jnp.exp(-0.5 * v * v) * density_norm
                cot = cbuf[p, c, rows16, cols].astype(f32)
                cbuf[p, c, rows16, cols] = (v * phi).astype(bf16)
                fbuf[p, c, rows16, cols] = (cot * (phi + v * density)).astype(bf16)
                return inner

            lax.fori_loop(0, chans, one, 0, unroll=4)
            return carry

        lax.fori_loop(0, halves * parts, piece, 0)
        store_out(p).start()
        store_gp(p).start()

    load(0).wait()
    analyse(0, 0)
    pl.semaphore_wait(barrier, nx + ny - 2)
    send_rows(0, 0)

    def first(p, carry):
        load(p).wait()
        analyse(0, p)
        send_rows(0, p)
        return carry

    lax.fori_loop(1, planes, first, 0)

    tx[...] = jnp.zeros_like(tx)
    for f, ref in enumerate((fx_ref, ix_ref)):
        for s in range(nx):
            for c in range(per):
                tx[f, pl.ds(s * LANES + c * slab, slab), pl.ds(c * modes, modes)] = ref[s, gy]

    tall = chans * PACK
    row = lax.broadcasted_iota(jnp.int32, (tall, chans), 0) // PACK
    col = lax.broadcasted_iota(jnp.int32, (tall, chans), 1)
    pick = jnp.where(row == col, 1.0, 0.0).astype(bf16)
    right = dot_t(lw_ref[...], pick, 1, 1).astype(bf16)
    left = dot_t(lw_ref[...], pick, 0, 1).astype(bf16)
    cut = 2 * LANES
    for k in range(tall // cut):
        sub = pick[k * cut:(k + 1) * cut]
        keep = (lax.broadcasted_iota(jnp.int32, (cut, tall), 0) % PACK
                == lax.broadcasted_iota(jnp.int32, (cut, tall), 1) % PACK)
        rows_k = pl.ds(k * cut, cut)
        kron_t[rows_k, :] = jnp.where(keep, jnp.dot(sub, right, preferred_element_type=f32), 0.0).astype(bf16)
        kron[rows_k, :] = jnp.where(keep, jnp.dot(sub, left, preferred_element_type=f32), 0.0).astype(bf16)
    store_kron().start()
    load_w().wait()

    def step(t, carry):
        def stage(lag, run):
            @pl.when((t >= lag) & (t < planes + lag))
            def _():
                run(t - lag)

        def middle(p):
            point(p)
            analyse(1, p)
            send_rows(1, p)

        stage(0, functools.partial(across, 0))
        stage(1, functools.partial(mix, 0))
        stage(2, functools.partial(expand, 0))
        stage(3, middle)
        stage(4, functools.partial(across, 1))
        stage(5, functools.partial(mix, 1))
        stage(6, functools.partial(expand, 1))
        return carry

    lax.fori_loop(0, planes + 6, step, 0)

    def finish(p, carry):
        for f in range(2):
            for o in range(1, nx):
                rows(f, p, o, True).wait_send()
                back(f, p, o, True).wait_send()
            for o in range(1, ny):
                sums(f, p, o, True).wait_send()
                mixed(f, p, o, True).wait_send()
        for o in range(1, nx):
            back(1, p, o, False).wait_recv()
        back_own(p).wait()
        store_out(p).wait()
        store_gp(p).wait()
        return carry

    lax.fori_loop(0, planes, finish, 0)
    store_kron().wait()


def main_pass(nx, ny, flow, cot, weight, local_weight, bias, fwd_y, inv_y, fwd_x, inv_x):
    planes, chans, slab, cells = flow.shape
    own, modes = weight.shape[0], weight.shape[3]
    per = LANES // slab
    groups = chans // per
    jg = modes // nx
    tall = chans * PACK
    vm = pl.BlockSpec(memory_space=pltpu.VMEM)
    hbm = pl.BlockSpec(memory_space=pl.ANY)
    dma = pltpu.SemaphoreType.DMA
    split = lambda t: t.reshape(nx, ny, slab, modes)
    field = jax.ShapeDtypeStruct(flow.shape, bf16)
    coef = jax.ShapeDtypeStruct((planes, own, chans, modes), bf16)
    return pl.pallas_call(
        functools.partial(main_kernel, nx, ny, planes, chans, slab, modes, own),
        out_shape=(
            field, field,
            jax.ShapeDtypeStruct((planes, groups, modes, LANES), bf16),
            jax.ShapeDtypeStruct((tall, tall), bf16),
            coef, coef,
        ),
        in_specs=[hbm, hbm, hbm, vm, pl.BlockSpec(memory_space=pltpu.SMEM), vm, vm, vm, vm],
        out_specs=(hbm, hbm, hbm, hbm, vm, vm),
        scratch_shapes=[
            pltpu.VMEM(flow.shape, bf16),
            pltpu.VMEM(flow.shape, bf16),
            pltpu.VMEM(weight.shape, bf16),
            pltpu.VMEM((2, nx * LANES, per * modes), bf16),
            pltpu.VMEM((tall, tall), bf16),
            pltpu.VMEM((tall, tall), bf16),
            pltpu.VMEM((2, planes, nx, groups, jg, LANES), bf16),
            pltpu.VMEM((2, planes, groups, jg, nx * LANES), bf16),
            pltpu.VMEM((chans * jg, modes), f32),
            pltpu.VMEM((2, planes, ny, own, chans, modes), bf16),
            pltpu.VMEM((2, planes, ny, own, chans, modes), bf16),
            pltpu.VMEM((own * chans, modes), f32),
            pltpu.VMEM((chans, modes), f32),
            pltpu.VMEM((2, planes, own, chans, modes), bf16),
            pltpu.VMEM((2, planes, ny, own, chans, modes), bf16),
            pltpu.VMEM((ny * own * chans, modes), f32),
            pltpu.VMEM((groups * jg, per * modes), bf16),
            pltpu.VMEM((2, planes, nx, groups, jg, LANES), bf16),
            pltpu.VMEM((planes, groups, modes, LANES), bf16),
            pltpu.VMEM((slab // PACK, tall, modes), bf16),
            pltpu.VMEM((chans, PACK, 2 * LANES), f32),
            pltpu.VMEM((tall, 2 * LANES), bf16),
            dma((planes,)), dma((planes,)), dma((2, planes)), dma, dma, dma((planes,)),
            dma((2, planes, nx)), dma((2, planes, nx)),
            dma((2, planes, ny)), dma((2, planes, ny)),
            dma((2, planes, ny)), dma((2, planes, ny)),
            dma((2, planes, nx)), dma((2, planes, nx)),
        ],
        compiler_params=pltpu.CompilerParams(
            collective_id=0, has_side_effects=True, vmem_limit_bytes=62 << 20),
        name="main_pass",
    )(flow, cot, weight, local_weight, bias, fwd_y.T, inv_y.T, split(fwd_x), split(inv_x))


def rows_by_half(g_ref, gt):
    groups = g_ref.shape[1]
    halves, tall, modes = gt.shape
    slab = halves * PACK
    per = LANES // slab

    def turn(g, carry):
        block = g_ref[0, g].T.reshape(per, halves, PACK, modes)
        for h in range(halves):
            gt[h, pl.ds(g * per * PACK, per * PACK), :] = block[:, h].reshape(per * PACK, modes)
        return carry

    lax.fori_loop(0, groups, turn, 0, unroll=4)


def backward_kernel(gp_ref, g_ref, yt_ref, kr_ref, co_ref, gm_ref, held_ref, out_ref, gs_ref, keep_ref, xs, gt, cf):
    _, chans, slab, width = gp_ref.shape
    planes, rows_here = co_ref.shape[0], co_ref.shape[1]

    @pl.when(pl.program_id(1) == 0)
    def _():
        rows_by_half(g_ref, gt)

    for h in range(slab // PACK):
        xs[...] = gp_ref[0, :, h * PACK:(h + 1) * PACK, :].reshape(chans * PACK, width)
        r = jnp.dot(kr_ref[...], xs[...], preferred_element_type=f32)
        r = r + jnp.dot(gt[h], yt_ref[...], preferred_element_type=f32)
        out_ref[0, :, h * PACK:(h + 1) * PACK, :] = r.reshape(chans, PACK, width).astype(bf16)

    keep_ref[...] = held_ref[...]
    cf[...] = co_ref[...].astype(f32).reshape(cf.shape)

    def outer(r, carry):
        total = cf[pl.ds(r, 1), :] * gm_ref[0, 0].astype(f32)
        for p in range(1, planes):
            total = total + cf[pl.ds(p * rows_here + r, 1), :] * gm_ref[p, 0].astype(f32)
        gs_ref[r] = total
        return carry

    lax.fori_loop(0, rows_here, outer, 0, unroll=4)


def backward_space(gp, g, table_y, kron, co, gm, held, parts):
    planes, chans, slab, cells = gp.shape
    groups, modes = g.shape[1], g.shape[2]
    own = co.shape[1]
    width = cells // parts
    rows_here = own * chans // (planes * parts)
    field = pl.BlockSpec((1, chans, slab, width), lambda p, h: (p, 0, 0, h))
    return pl.pallas_call(
        backward_kernel,
        grid=(planes, parts),
        out_shape=(
            jax.ShapeDtypeStruct(gp.shape, bf16),
            jax.ShapeDtypeStruct((own * chans, chans, modes), f32),
            jax.ShapeDtypeStruct(gp.shape, bf16),
        ),
        in_specs=[
            field,
            pl.BlockSpec((1, groups, modes, LANES), lambda p, h: (p, 0, 0, 0)),
            pl.BlockSpec((modes, width), lambda p, h: (0, h)),
            pl.BlockSpec(kron.shape, lambda p, h: (0, 0), pipeline_mode=pl.Buffered(1)),
            pl.BlockSpec((planes, rows_here, modes), lambda p, h: (0, p * parts + h, 0)),
            pl.BlockSpec((planes, 1, chans, modes), lambda p, h: (0, (p * parts + h) * rows_here // chans, 0, 0)),
            field,
        ],
        out_specs=(field, pl.BlockSpec((rows_here, chans, modes), lambda p, h: (p * parts + h, 0, 0)), field),
        scratch_shapes=[
            pltpu.VMEM((chans * PACK, width), bf16),
            pltpu.VMEM((slab // PACK, chans * PACK, modes), bf16),
            pltpu.VMEM((planes * rows_here, modes), f32),
        ],
        compiler_params=pltpu.CompilerParams(vmem_limit_bytes=56 << 20),
        name="backward_space",
    )(gp, g, table_y.T, kron, co.reshape(planes, own * chans, modes), gm, held)


def kernel_shards(nx, ny, flow_field, cotangent, spectral_weight, local_weight, channel_bias):
    planes, chans, slab, cells = flow_field.shape
    across = slab * nx * ny
    own, modes = spectral_weight.shape[0], spectral_weight.shape[3]
    scale_inv = math.sqrt(1.0 / (modes // 2))
    fwd_x = basis_table(across, modes, math.sqrt(2.0 / across))
    fwd_y = basis_table(cells, modes, math.sqrt(2.0 / cells))
    inv_x = basis_table(across, modes, scale_inv)
    inv_y = basis_table(cells, modes, scale_inv)
    out, grad_pre, back, kron, coeffs, grad_mixed = main_pass(
        nx, ny, flow_field, cotangent, spectral_weight, local_weight, channel_bias, fwd_y, inv_y, fwd_x, inv_x)
    grad_field, grad_spectral, out = backward_space(grad_pre, back, fwd_y, kron, coeffs, grad_mixed, out, 2)
    return out, grad_field, grad_spectral.reshape(own, chans, chans, modes)


def solution(mesh):
    nx, ny = mesh.shape["gx"], mesh.shape["gy"]

    def shards(flow_field, cotangent, spectral_weight, local_weight, channel_bias):
        planes, chans, slab, cells = flow_field.shape
        own, modes = spectral_weight.shape[0], spectral_weight.shape[3]
        fits = (
            slab % PACK == 0 and LANES % slab == 0 and modes == LANES
            and nx % 2 == 0 and (modes // nx) % PACK == 0
            and chans % (2 * LANES // slab) == 0 and chans % PACK == 0
            and cells % (2 * LANES) == 0
            and own * nx * ny == modes and chans % (own * chans // (2 * planes)) == 0
        )
        args = (flow_field, cotangent, spectral_weight, local_weight, channel_bias)
        return kernel_shards(nx, ny, *args) if fits else plain_shards(*args)

    placed = (
        P(None, None, ("gx", "gy"), None),
        P(None, None, ("gx", "gy"), None),
        P(("gx", "gy"), None, None, None),
        P(),
        P(),
    )
    return jax.shard_map(
        shards,
        mesh=mesh,
        in_specs=placed,
        out_specs=(
            P(None, None, ("gx", "gy"), None),
            P(None, None, ("gx", "gy"), None),
            P(("gx", "gy"), None, None, None),
        ),
        check_vma=False,
    )
```

profile of v0, /device:TPU:25, one launch (start us, length us, event | category | flops | bytes accessed | tf_op | source)
XLA Modules:
  0.0 159.5 jit_solution(2030240399192524404)
XLA Ops:
  0.6 135.1 %main_pass.1 = (bf16[4,64,32,512]{3,2,1,0:T(8,128)(2,1)}, bf16[4,64,32,512]{3,2,1,0:T(8,128)(2,1)}, bf16[4,16,128,128]{3,2,1,0:T(8,128)(2,1)}, bf16[1024,1024]{1...) custom-call(bf16[4,64,32,512]{3,2,1,0:T(8,128)(2,1)} %flow_hbm.1, ...), custom_call_target="tpu_custom_call" | custom-call | tf_op jit(solution)/shard_map/main_pass/pallas_call | solution.py:398
  135.7 23.7 %backward_space.1 = (bf16[4,64,32,512]{3,2,1,0:T(8,128)(2,1)}, f32[256,64,128]{2,1,0:T(8,128)}, bf16[4,64,32,512]{3,2,1,0:T(8,128)(2,1)}) custom-call(bf16[4,64,32,512]{3,2,1,0:T(8,128)(2,1)} %get-tuple-element.12.gp_ref, bf16[4,16,128,128]{3,2,1,0:T(8,128)(2,1)} %get-tuple-element.13.g_ref, bf16[128,512]{1,0:T(8,128)(2,1)} %constant.13.fy_ref.yt_ref, ...), custom_call_target="tpu_custom_call" | custom-call | tf_op jit(solution)/shard_map/backward_space/pallas_call | solution.py:492
where the time goes:
time: 160 us; the launch traced here: 159 us
  Pallas kernels  159 us (99%)
    pallas_call x1, Pallas kernels, main_pass(): pl.pallas_call(functools.partial(main_kernel, nx, ny, planes, chans, slab...  135 us
    pallas_call x1, Pallas kernels, backward_space(): pl.pallas_call(backward_kernel, grid=(planes, parts), out_shape=(jax.Shap...  23.7 us

commit v1 on v0

--- a/solution.py
+++ b/solution.py
@@ -98,10 +98,10 @@
 def main_kernel(
     nx, ny, planes, chans, slab, modes, own,
     flow_hbm, cot_hbm, w_hbm, lw_ref, bias_ref, fy_ref, iy_ref, fx_ref, ix_ref,
-    out_hbm, gp_hbm, back_hbm, kron_hbm, co_ref, gm_ref,
-    fbuf, cbuf, wbuf, tx, kron, kron_t, sbuf, rbuf, part, zs, zr, cf, gf, ms, zg, tg, lhs2, isb,
+    cbuf, fbuf, back_ref, co_ref, gm_ref,
+    wbuf, tx, kron, kron_t, sbuf, rbuf, part, zs, zr, cf, gf, ms, zg, tg, lhs2, isb,
     gbuf, gt, pre, xs,
-    load_sem, cot_sem, store_sem, w_sem, kron_sem, own_sem, s1, r1, s2, r2, s3, r3, s4, r4,
+    load_sem, cot_sem, w_sem, s1, r1, s2, r2, s3, r3, s4, r4,
 ):
     gx, gy = lax.axis_index("gx"), lax.axis_index("gy")
     per = LANES // slab
@@ -118,17 +118,8 @@
     def load_cot(p):
         return pltpu.make_async_copy(cot_hbm.at[p], cbuf.at[p], cot_sem.at[p])
 
-    def store_out(p):
-        return pltpu.make_async_copy(cbuf.at[p], out_hbm.at[p], store_sem.at[0, p])
-
-    def store_gp(p):
-        return pltpu.make_async_copy(fbuf.at[p], gp_hbm.at[p], store_sem.at[1, p])
-
     def load_w():
         return pltpu.make_async_copy(w_hbm, wbuf, w_sem)
-
-    def store_kron():
-        return pltpu.make_async_copy(kron_t, kron_hbm, kron_sem)
 
     for p in range(planes):
         load(p).start()
@@ -172,13 +163,10 @@
     def back(f, p, o, out):
         other = (gx + o) % nx if out else (gx + nx - o) % nx
         slot = gx if out else other
-        into = back_hbm if f else gbuf
+        into = back_ref if f else gbuf
         return pltpu.make_async_remote_copy(
             isb.at[f, p, other], into.at[p, :, jrows(slot), :], s4.at[f, p, o], r4.at[f, p, o],
             device_id=(other, gy), device_id_type=MESH)
-
-    def back_own(p):
-        return pltpu.make_async_copy(isb.at[1, p, gx], back_hbm.at[p, :, jrows(gx), :], own_sem.at[p])
 
     def analyse(f, p):
         table = iy_ref if f else fy_ref
@@ -260,10 +248,8 @@
             return carry
 
         lax.fori_loop(0, nx // 2, body, 0, unroll=2)
-        if f:
-            back_own(p).start()
-        else:
-            gbuf[p, :, jrows(gx), :] = isb[f, p, gx]
+        into = back_ref if f else gbuf
+        into[p, :, jrows(gx), :] = isb[f, p, gx]
         for o in range(1, nx):
             back(f, p, o, True).start()
 
@@ -302,8 +288,18 @@
             return carry
 
         lax.fori_loop(0, halves * parts, piece, 0)
-        store_out(p).start()
-        store_gp(p).start()
+
+    def through(p):
+        def piece(s, carry):
+            h, y = s // parts, s % parts
+            rows16 = pl.ds(pl.multiple_of(h * PACK, PACK), PACK)
+            cols = pl.ds(pl.multiple_of(y * width, width), width)
+            xs[...] = fbuf[p, :, rows16, cols].reshape(chans * PACK, width)
+            r = jnp.dot(kron_t[...], xs[...], preferred_element_type=f32)
+            fbuf[p, :, rows16, cols] = r.astype(bf16).reshape(chans, PACK, width)
+            return carry
+
+        lax.fori_loop(0, halves * parts, piece, 0)
 
     load(0).wait()
     analyse(0, 0)
@@ -338,7 +334,6 @@
         rows_k = pl.ds(k * cut, cut)
         kron_t[rows_k, :] = jnp.where(keep, jnp.dot(sub, right, preferred_element_type=f32), 0.0).astype(bf16)
         kron[rows_k, :] = jnp.where(keep, jnp.dot(sub, left, preferred_element_type=f32), 0.0).astype(bf16)
-    store_kron().start()
     load_w().wait()
 
     def step(t, carry):
@@ -359,6 +354,7 @@
         stage(4, functools.partial(across, 1))
         stage(5, functools.partial(mix, 1))
         stage(6, functools.partial(expand, 1))
+        stage(6, through)
         return carry
 
     lax.fori_loop(0, planes + 6, step, 0)
@@ -373,13 +369,9 @@
                 mixed(f, p, o, True).wait_send()
         for o in range(1, nx):
             back(1, p, o, False).wait_recv()
-        back_own(p).wait()
-        store_out(p).wait()
-        store_gp(p).wait()
         return carry
 
     lax.fori_loop(0, planes, finish, 0)
-    store_kron().wait()
 
 
 def main_pass(nx, ny, flow, cot, weight, local_weight, bias, fwd_y, inv_y, fwd_x, inv_x):
@@ -393,21 +385,18 @@
     hbm = pl.BlockSpec(memory_space=pl.ANY)
     dma = pltpu.SemaphoreType.DMA
     split = lambda t: t.reshape(nx, ny, slab, modes)
-    field = jax.ShapeDtypeStruct(flow.shape, bf16)
-    coef = jax.ShapeDtypeStruct((planes, own, chans, modes), bf16)
+    field = pltpu.VMEM(flow.shape, bf16)
+    coef = pltpu.VMEM((planes, own, chans, modes), bf16)
     return pl.pallas_call(
         functools.partial(main_kernel, nx, ny, planes, chans, slab, modes, own),
         out_shape=(
             field, field,
-            jax.ShapeDtypeStruct((planes, groups, modes, LANES), bf16),
-            jax.ShapeDtypeStruct((tall, tall), bf16),
+            pltpu.VMEM((planes, groups, modes, LANES), bf16),
             coef, coef,
         ),
         in_specs=[hbm, hbm, hbm, vm, pl.BlockSpec(memory_space=pltpu.SMEM), vm, vm, vm, vm],
-        out_specs=(hbm, hbm, hbm, hbm, vm, vm),
+        out_specs=(vm, vm, vm, vm, vm),
         scratch_shapes=[
-            pltpu.VMEM(flow.shape, bf16),
-            pltpu.VMEM(flow.shape, bf16),
             pltpu.VMEM(weight.shape, bf16),
             pltpu.VMEM((2, nx * LANES, per * modes), bf16),
             pltpu.VMEM((tall, tall), bf16),
@@ -428,26 +417,26 @@
             pltpu.VMEM((slab // PACK, tall, modes), bf16),
             pltpu.VMEM((chans, PACK, 2 * LANES), f32),
             pltpu.VMEM((tall, 2 * LANES), bf16),
-            dma((planes,)), dma((planes,)), dma((2, planes)), dma, dma, dma((planes,)),
+            dma((planes,)), dma((planes,)), dma,
             dma((2, planes, nx)), dma((2, planes, nx)),
             dma((2, planes, ny)), dma((2, planes, ny)),
             dma((2, planes, ny)), dma((2, planes, ny)),
             dma((2, planes, nx)), dma((2, planes, nx)),
         ],
         compiler_params=pltpu.CompilerParams(
-            collective_id=0, has_side_effects=True, vmem_limit_bytes=62 << 20),
+            collective_id=0, has_side_effects=True, vmem_limit_bytes=40 << 20),
         name="main_pass",
     )(flow, cot, weight, local_weight, bias, fwd_y.T, inv_y.T, split(fwd_x), split(inv_x))
 
 
-def rows_by_half(g_ref, gt):
+def rows_by_half(g_ref, p, gt):
     groups = g_ref.shape[1]
     halves, tall, modes = gt.shape
     slab = halves * PACK
     per = LANES // slab
 
     def turn(g, carry):
-        block = g_ref[0, g].T.reshape(per, halves, PACK, modes)
+        block = g_ref[p, g].T.reshape(per, halves, PACK, modes)
         for h in range(halves):
             gt[h, pl.ds(g * per * PACK, per * PACK), :] = block[:, h].reshape(per * PACK, modes)
         return carry
@@ -455,66 +444,76 @@
     lax.fori_loop(0, groups, turn, 0, unroll=4)
 
 
-def backward_kernel(gp_ref, g_ref, yt_ref, kr_ref, co_ref, gm_ref, held_ref, out_ref, gs_ref, keep_ref, xs, gt, cf):
-    _, chans, slab, width = gp_ref.shape
-    planes, rows_here = co_ref.shape[0], co_ref.shape[1]
-
-    @pl.when(pl.program_id(1) == 0)
+def last_kernel(thru_ref, g_ref, yt_ref, co_ref, gm_ref, held_ref, out_ref, gs_ref, keep_hbm, gt, cf, sem):
+    _, chans, slab, width = out_ref.shape
+    planes, own = co_ref.shape[:2]
+    rows_here = gs_ref.shape[0]
+    p, part = pl.program_id(0), pl.program_id(1)
+
+    def keep(q):
+        return pltpu.make_async_copy(held_ref.at[q], keep_hbm.at[q], sem.at[q])
+
+    @pl.when(part == 0)
     def _():
-        rows_by_half(g_ref, gt)
-
+        keep(p).start()
+        rows_by_half(g_ref, p, gt)
+
+    cols = pl.ds(pl.multiple_of(part * width, width), width)
     for h in range(slab // PACK):
-        xs[...] = gp_ref[0, :, h * PACK:(h + 1) * PACK, :].reshape(chans * PACK, width)
-        r = jnp.dot(kr_ref[...], xs[...], preferred_element_type=f32)
-        r = r + jnp.dot(gt[h], yt_ref[...], preferred_element_type=f32)
-        out_ref[0, :, h * PACK:(h + 1) * PACK, :] = r.reshape(chans, PACK, width).astype(bf16)
-
-    keep_ref[...] = held_ref[...]
-    cf[...] = co_ref[...].astype(f32).reshape(cf.shape)
+        r = jnp.dot(gt[h], yt_ref[...], preferred_element_type=f32).reshape(chans, PACK, width)
+        r = r + thru_ref[p, :, h * PACK:(h + 1) * PACK, cols].astype(f32)
+        out_ref[0, :, h * PACK:(h + 1) * PACK, :] = r.astype(bf16)
+
+    first = (p * pl.num_programs(1) + part) * rows_here
+    j, i = first // chans, pl.multiple_of(first % chans, rows_here)
+    cf[...] = co_ref[:, j, pl.ds(i, rows_here), :].astype(f32).reshape(cf.shape)
 
     def outer(r, carry):
-        total = cf[pl.ds(r, 1), :] * gm_ref[0, 0].astype(f32)
-        for p in range(1, planes):
-            total = total + cf[pl.ds(p * rows_here + r, 1), :] * gm_ref[p, 0].astype(f32)
+        total = cf[pl.ds(r, 1), :] * gm_ref[0, j].astype(f32)
+        for q in range(1, planes):
+            total = total + cf[pl.ds(q * rows_here + r, 1), :] * gm_ref[q, j].astype(f32)
         gs_ref[r] = total
         return carry
 
     lax.fori_loop(0, rows_here, outer, 0, unroll=4)
 
-
-def backward_space(gp, g, table_y, kron, co, gm, held, parts):
-    planes, chans, slab, cells = gp.shape
-    groups, modes = g.shape[1], g.shape[2]
-    own = co.shape[1]
+    @pl.when((p == planes - 1) & (part == pl.num_programs(1) - 1))
+    def _():
+        for q in range(planes):
+            keep(q).wait()
+
+
+def last_pass(thru, g, table_y, co, gm, held, parts):
+    planes, chans, slab, cells = thru.shape
+    modes, own = g.shape[2], co.shape[1]
     width = cells // parts
     rows_here = own * chans // (planes * parts)
     field = pl.BlockSpec((1, chans, slab, width), lambda p, h: (p, 0, 0, h))
+    whole = pl.BlockSpec(memory_space=pltpu.VMEM)
+    shape = jax.ShapeDtypeStruct(thru.shape, bf16)
     return pl.pallas_call(
-        backward_kernel,
+        last_kernel,
         grid=(planes, parts),
-        out_shape=(
-            jax.ShapeDtypeStruct(gp.shape, bf16),
-            jax.ShapeDtypeStruct((own * chans, chans, modes), f32),
-            jax.ShapeDtypeStruct(gp.shape, bf16),
+        out_shape=(shape, jax.ShapeDtypeStruct((own * chans, chans, modes), f32), shape),
+        in_specs=[
+            whole,
+            whole,
+            pl.BlockSpec((modes, width), lambda p, h: (0, h)),
+            whole, whole, whole,
+        ],
+        out_specs=(
+            field,
+            pl.BlockSpec((rows_here, chans, modes), lambda p, h: (p * parts + h, 0, 0)),
+            pl.BlockSpec(memory_space=pl.ANY),
         ),
-        in_specs=[
-            field,
-            pl.BlockSpec((1, groups, modes, LANES), lambda p, h: (p, 0, 0, 0)),
-            pl.BlockSpec((modes, width), lambda p, h: (0, h)),
-            pl.BlockSpec(kron.shape, lambda p, h: (0, 0), pipeline_mode=pl.Buffered(1)),
-            pl.BlockSpec((planes, rows_here, modes), lambda p, h: (0, p * parts + h, 0)),
-            pl.BlockSpec((planes, 1, chans, modes), lambda p, h: (0, (p * parts + h) * rows_here // chans, 0, 0)),
-            field,
-        ],
-        out_specs=(field, pl.BlockSpec((rows_here, chans, modes), lambda p, h: (p * parts + h, 0, 0)), field),
         scratch_shapes=[
-            pltpu.VMEM((chans * PACK, width), bf16),
             pltpu.VMEM((slab // PACK, chans * PACK, modes), bf16),
             pltpu.VMEM((planes * rows_here, modes), f32),
+            pltpu.SemaphoreType.DMA((planes,)),
         ],
-        compiler_params=pltpu.CompilerParams(vmem_limit_bytes=56 << 20),
-        name="backward_space",
-    )(gp, g, table_y.T, kron, co.reshape(planes, own * chans, modes), gm, held)
+        compiler_params=pltpu.CompilerParams(vmem_limit_bytes=20 << 20),
+        name="last_pass",
+    )(thru, g, table_y.T, co, gm, held)
 
 
 def kernel_shards(nx, ny, flow_field, cotangent, spectral_weight, local_weight, channel_bias):
@@ -526,9 +525,9 @@
     fwd_y = basis_table(cells, modes, math.sqrt(2.0 / cells))
     inv_x = basis_table(across, modes, scale_inv)
     inv_y = basis_table(cells, modes, scale_inv)
-    out, grad_pre, back, kron, coeffs, grad_mixed = main_pass(
+    out, thru, back, coeffs, grad_mixed = main_pass(
         nx, ny, flow_field, cotangent, spectral_weight, local_weight, channel_bias, fwd_y, inv_y, fwd_x, inv_x)
-    grad_field, grad_spectral, out = backward_space(grad_pre, back, fwd_y, kron, coeffs, grad_mixed, out, 2)
+    grad_field, grad_spectral, out = last_pass(thru, back, fwd_y, coeffs, grad_mixed, out, 2)
     return out, grad_field, grad_spectral.reshape(own, chans, chans, modes)
 
 

time: 160 us -> 145 us (0.906)
  Pallas kernels: 159 us -> 145 us
    pallas_call x1, Pallas kernels: 23.7 us -> 10.6 us  [last_pass(): pl.pallas_call(last_kernel, grid=(planes, parts), out_shape=(shape, jax.S...]
where the time goes in v1:
time: 145 us
  Pallas kernels  145 us (100%)
    pallas_call x1, Pallas kernels, main_pass(): pl.pallas_call(functools.partial(main_kernel, nx, ny, planes, chans, slab...  134 us
    pallas_call x1, Pallas kernels, last_pass(): pl.pallas_call(last_kernel, grid=(planes, parts), out_shape=(shape, jax.S...  10.6 us

profile of v1, /device:TPU:25, one launch (start us, length us, event | category | flops | bytes accessed | tf_op | source)
XLA Modules:
  0.0 145.3 jit_solution(17492190471217816797)
XLA Ops:
  0.6 0.0 copy-start
  0.6 134.0 %main_pass.1 = (bf16[4,64,32,512]{3,2,1,0:T(8,128)(2,1)S(1)}, bf16[4,64,32,512]{3,2,1,0:T(8,128)(2,1)S(1)}, bf16[4,16,128,128]{3,2,1,0:T(8,128)(2,1)S(1)}, bf16[...) custom-call(bf16[4,64,32,512]{3,2,1,0:T(8,128)(2,1)} %flow_hbm.1, bf16[4,64,32,512]{3,2,1,0:T(8,128)(2,1)} %cot_hbm.1, ...), custom_call_target="tpu_custom_call" | custom-call | tf_op jit(solution)/shard_map/main_pass/pallas_call | solution.py:390
  134.7 0.0 copy-done
  134.7 10.6 %last_pass.1 = (bf16[4,64,32,512]{3,2,1,0:T(8,128)(2,1)}, f32[256,64,128]{2,1,0:T(8,128)}, bf16[4,64,32,512]{3,2,1,0:T(8,128)(2,1)}) custom-call(bf16[4,64,32,512]{3,2,1,0:T(8,128)(2,1)S(1)} %get-tuple-element.11.thru_ref, bf16[4,16,128,128]{3,2,1,0:T(8,128)(2,1)S(1)} %get-tuple-element.12.g_ref, bf16[128,512]{1,0:T(8,128)(2,1)S(1)} %copy-done, ...), custom_call_target="tpu_custom_call" | custom-call | tf_op jit(solution)/shard_map/last_pass/pallas_call | solution.py:494
Async XLA Ops:
  0.6 134.1 %copy-start = (bf16[128,512]{1,0:T(8,128)(2,1)S(1)}, bf16[128,512]{1,0:T(8,128)(2,1)}, u32[]{:S(2)}) copy-start(bf16[128,512]{1,0:T(8,128)(2,1)} %constant.13.fy_ref.yt_ref) | copy-start | bytes 393220

commit v2 on v1

--- a/solution.py
+++ b/solution.py
@@ -99,7 +99,7 @@
     nx, ny, planes, chans, slab, modes, own,
     flow_hbm, cot_hbm, w_hbm, lw_ref, bias_ref, fy_ref, iy_ref, fx_ref, ix_ref,
     cbuf, fbuf, back_ref, co_ref, gm_ref,
-    wbuf, tx, kron, kron_t, sbuf, rbuf, part, zs, zr, cf, gf, ms, zg, tg, lhs2, isb,
+    wbuf, tx, kron, kron_t, sbuf, rbuf, part, zs, zr, zq, cf, ms, zg, tg, lhs2, isb,
     gbuf, gt, pre, xs,
     load_sem, cot_sem, w_sem, s1, r1, s2, r2, s3, r3, s4, r4,
 ):
@@ -146,19 +146,90 @@
             sbuf.at[f, p, other], rbuf.at[f, p, :, :, lane(slot)], s1.at[f, p, o], r1.at[f, p, o],
             device_id=(other, gy), device_id_type=MESH)
 
-    def sums(f, p, o, out):
-        other = (gy + o) % ny if out else (gy + ny - o) % ny
-        slot = gy if out else other
+    side = gy // 2
+    outer, inner = 3 * side, 1 + side
+    far_inner, far_outer = 2 - side, 3 - 3 * side
+    partner = outer + inner - gy
+    at_inner = gy == inner
+    at_outer = gy != inner
+
+    def along(f, p, src, dst, to, sent, got):
         return pltpu.make_async_remote_copy(
-            zs.at[f, p, other], zr.at[f, p, slot], s2.at[f, p, o], r2.at[f, p, o],
-            device_id=(gx, other), device_id_type=MESH)
-
-    def mixed(f, p, o, out):
-        other = (gy + o) % ny if out else (gy + ny - o) % ny
-        slot = gy if out else other
-        return pltpu.make_async_remote_copy(
-            ms.at[f, p], zg.at[f, p, slot], s3.at[f, p, o], r3.at[f, p, o],
-            device_id=(gx, other), device_id_type=MESH)
+            src, dst, sent, got, device_id=(gx, to), device_id_type=MESH)
+
+    def sums_near(f, p, i, dest, to):
+        return along(f, p, zs.at[f, p, dest], zr.at[f, p, i], to, s2.at[f, p, i], r2.at[f, p, i])
+
+    def sums_far(f, p, i, to):
+        return along(f, p, zq.at[f, p, i], zr.at[f, p, 3], to, s2.at[f, p, 1 + i], r2.at[f, p, 3])
+
+    def mixed_near(f, p, i, slot, to):
+        return along(f, p, ms.at[f, p], zg.at[f, p, slot], to, s3.at[f, p, i], r3.at[f, p, slot])
+
+    def mixed_on(f, p, i, slot, to):
+        return along(f, p, zg.at[f, p, slot], zg.at[f, p, slot], to, s3.at[f, p, 2 + i], r3.at[f, p, slot])
+
+    def send_sums(f, p):
+        @pl.when(at_outer)
+        def _():
+            for i, dest in enumerate((inner, far_inner, far_outer)):
+                sums_near(f, p, i, dest, inner).start()
+
+        @pl.when(at_inner)
+        def _():
+            sums_near(f, p, 0, outer, outer).start()
+
+    def relay_sums(f, p):
+        @pl.when(at_inner)
+        def _():
+            for i in range(3):
+                sums_near(f, p, i, gy, outer).wait_recv()
+            for i, dest in enumerate((far_inner, far_outer)):
+                zq[f, p, i] = (zr[f, p, 1 + i].astype(f32) + zs[f, p, dest].astype(f32)).astype(bf16)
+                sums_far(f, p, i, dest).start()
+
+    def take_sums(f, p):
+        @pl.when(at_outer)
+        def _():
+            sums_near(f, p, 0, gy, inner).wait_recv()
+
+        sums_far(f, p, 0, far_inner).wait_recv()
+        return zs[f, p, gy].astype(f32) + zr[f, p, 0].astype(f32) + zr[f, p, 3].astype(f32)
+
+    def send_mixed(f, p):
+        mixed_near(f, p, 0, gy, partner).start()
+        mixed_near(f, p, 1, gy, far_inner).start()
+
+    def relay_mixed(f, p):
+        @pl.when(at_inner)
+        def _():
+            for i, slot in enumerate((far_inner, far_outer)):
+                mixed_near(f, p, i, slot, slot).wait_recv()
+                mixed_on(f, p, i, slot, outer).start()
+
+    def take_mixed(f, p):
+        mixed_near(f, p, 0, partner, partner).wait_recv()
+
+        @pl.when(at_outer)
+        def _():
+            for i, slot in enumerate((far_inner, far_outer)):
+                mixed_on(f, p, i, slot, inner).wait_recv()
+
+    def gy_sent(f, p):
+        @pl.when(at_outer)
+        def _():
+            for i, dest in enumerate((inner, far_inner, far_outer)):
+                sums_near(f, p, i, dest, inner).wait_send()
+
+        @pl.when(at_inner)
+        def _():
+            sums_near(f, p, 0, outer, outer).wait_send()
+            for i, dest in enumerate((far_inner, far_outer)):
+                sums_far(f, p, i, dest).wait_send()
+                mixed_on(f, p, i, dest, outer).wait_send()
+
+        mixed_near(f, p, 0, gy, partner).wait_send()
+        mixed_near(f, p, 1, gy, far_inner).wait_send()
 
     def back(f, p, o, out):
         other = (gx + o) % nx if out else (gx + nx - o) % nx
@@ -171,14 +242,16 @@
     def analyse(f, p):
         table = iy_ref if f else fy_ref
 
+        wide = groups // 2
+
         def body(t, carry):
-            x = fbuf[p, pl.ds(t * 2 * per, 2 * per)].reshape(2 * LANES, cells)
+            x = fbuf[p, pl.ds(t * wide * per, wide * per)].reshape(wide * LANES, cells)
             r = dot_t(table[...], x, 1, 1).astype(bf16)
-            for h in range(2):
-                sbuf[f, p, :, t * 2 + h] = r[:, h * LANES:(h + 1) * LANES].reshape(nx, jg, LANES)
+            for h in range(wide):
+                sbuf[f, p, :, t * wide + h] = r[:, h * LANES:(h + 1) * LANES].reshape(nx, jg, LANES)
             return carry
 
-        lax.fori_loop(0, groups // 2, body, 0, unroll=2)
+        lax.fori_loop(0, 2, body, 0)
         rbuf[f, p, :, :, lane(gx)] = sbuf[f, p, gx]
 
     def send_rows(f, p):
@@ -195,17 +268,10 @@
                 part[pl.ds((g * per + c) * jg, jg), :] = r[g * jg:(g + 1) * jg, c * modes:(c + 1) * modes]
         for j in range(jg):
             zs[f, p, j // own, j % own] = part[pl.ds(j, chans, stride=jg), :].astype(bf16)
-        zr[f, p, gy] = zs[f, p, gy]
-        for o in range(1, ny):
-            sums(f, p, o, True).start()
+        send_sums(f, p)
 
     def mix(f, p):
-        for o in range(1, ny):
-            sums(f, p, o, False).wait_recv()
-        total = zr[f, p, 0].astype(f32)
-        for s in range(1, ny):
-            total = total + zr[f, p, s].astype(f32)
-        coef = total.astype(bf16)
+        coef = take_sums(f, p).astype(bf16)
         if f:
             gm_ref[p] = coef
         else:
@@ -217,11 +283,14 @@
 
                 def body(i, carry):
                     prod = wbuf[j, i].astype(f32) * right
-                    gf[pl.ds(i, 1), :] = jnp.sum(prod, axis=0, keepdims=True)
+                    part[pl.ds(pl.multiple_of(i * 8, 8), 8), :] = jnp.sum(prod.reshape(chans // 8, 8, modes), axis=0)
                     return carry
 
                 lax.fori_loop(0, chans, body, 0, unroll=8)
-                ms[f, p, j] = gf[...].astype(bf16)
+                total = part[pl.ds(0, chans, stride=8), :]
+                for k in range(1, 8):
+                    total = total + part[pl.ds(k, chans, stride=8), :]
+                ms[f, p, j] = total.astype(bf16)
             else:
 
                 def body(i, acc):
@@ -230,12 +299,10 @@
                 acc = lax.fori_loop(0, chans, body, jnp.zeros((chans, modes), f32), unroll=8)
                 ms[f, p, j] = acc.astype(bf16)
         zg[f, p, gy] = ms[f, p]
-        for o in range(1, ny):
-            mixed(f, p, o, True).start()
+        send_mixed(f, p)
 
     def expand(f, p):
-        for o in range(1, ny):
-            mixed(f, p, o, False).wait_recv()
+        take_mixed(f, p)
         tg[...] = zg[f, p].astype(f32).reshape(ny * own * chans, modes)
         for c in range(chans):
             lhs2[pl.ds((c // per) * jg, jg), pl.ds((c % per) * modes, modes)] = tg[pl.ds(c, jg, stride=chans), :].astype(bf16)
@@ -253,7 +320,7 @@
         for o in range(1, nx):
             back(f, p, o, True).start()
 
-    def point(p):
+    def open_point(p):
         load_cot(p).wait()
         for o in range(1, nx):
             back(0, p, o, False).wait_recv()
@@ -266,6 +333,7 @@
 
         lax.fori_loop(0, groups, turn, 0, unroll=4)
 
+    def pieces(lo, hi, p):
         def piece(s, carry):
             h, y = s // parts, s % parts
             rows16 = pl.ds(pl.multiple_of(h * PACK, PACK), PACK)
@@ -284,10 +352,21 @@
                 fbuf[p, c, rows16, cols] = (cot * (phi + v * density)).astype(bf16)
                 return inner
 
-            lax.fori_loop(0, chans, one, 0, unroll=4)
+            lax.fori_loop(0, chans, one, 0, unroll=8)
             return carry
 
-        lax.fori_loop(0, halves * parts, piece, 0)
+        lax.fori_loop(lo, hi, piece, 0)
+
+    total = halves * parts
+
+    def point_part(i, p):
+        if i == 0:
+            open_point(p)
+        pieces(i * total // 2, (i + 1) * total // 2, p)
+
+    def turn_home(p):
+        analyse(1, p)
+        send_rows(1, p)
 
     def through(p):
         def piece(s, carry):
@@ -342,31 +421,38 @@
             def _():
                 run(t - lag)
 
-        def middle(p):
-            point(p)
-            analyse(1, p)
-            send_rows(1, p)
-
-        stage(0, functools.partial(across, 0))
-        stage(1, functools.partial(mix, 0))
-        stage(2, functools.partial(expand, 0))
-        stage(3, middle)
-        stage(4, functools.partial(across, 1))
-        stage(5, functools.partial(mix, 1))
-        stage(6, functools.partial(expand, 1))
-        stage(6, through)
+        for lag, run in plan:
+            stage(lag, run)
         return carry
 
-    lax.fori_loop(0, planes + 6, step, 0)
+    forth = lambda fn: functools.partial(fn, 0)
+    home = lambda fn: functools.partial(fn, 1)
+    half = lambda i: functools.partial(point_part, i)
+    plan = (
+        (0, forth(across)),
+        (6, home(across)),
+        (8, home(relay_mixed)),
+        (7, home(mix)),
+        (10, through),
+        (1, forth(relay_sums)),
+        (3, forth(expand)),
+        (4, half(0)),
+        (6, home(relay_sums)),
+        (2, forth(relay_mixed)),
+        (4, half(1)),
+        (4, turn_home),
+        (8, home(expand)),
+        (1, forth(mix)),
+    )
+
+    lax.fori_loop(0, planes + max(lag for lag, _ in plan), step, 0)
 
     def finish(p, carry):
         for f in range(2):
             for o in range(1, nx):
                 rows(f, p, o, True).wait_send()
                 back(f, p, o, True).wait_send()
-            for o in range(1, ny):
-                sums(f, p, o, True).wait_send()
-                mixed(f, p, o, True).wait_send()
+            gy_sent(f, p)
         for o in range(1, nx):
             back(1, p, o, False).wait_recv()
         return carry
@@ -406,8 +492,8 @@
             pltpu.VMEM((chans * jg, modes), f32),
             pltpu.VMEM((2, planes, ny, own, chans, modes), bf16),
             pltpu.VMEM((2, planes, ny, own, chans, modes), bf16),
+            pltpu.VMEM((2, planes, 2, own, chans, modes), bf16),
             pltpu.VMEM((own * chans, modes), f32),
-            pltpu.VMEM((chans, modes), f32),
             pltpu.VMEM((2, planes, own, chans, modes), bf16),
             pltpu.VMEM((2, planes, ny, own, chans, modes), bf16),
             pltpu.VMEM((ny * own * chans, modes), f32),
@@ -539,7 +625,7 @@
         own, modes = spectral_weight.shape[0], spectral_weight.shape[3]
         fits = (
             slab % PACK == 0 and LANES % slab == 0 and modes == LANES
-            and nx % 2 == 0 and (modes // nx) % PACK == 0
+            and nx % 2 == 0 and ny == 4 and (modes // nx) % PACK == 0
             and chans % (2 * LANES // slab) == 0 and chans % PACK == 0
             and cells % (2 * LANES) == 0
             and own * nx * ny == modes and chans % (own * chans // (2 * planes)) == 0

time: 145 us -> 139 us (0.959); the launches traced: 145 us -> 136 us
  Pallas kernels: 145 us -> 135 us
    pallas_call x1, Pallas kernels: 134 us -> 125 us  [main_pass(): pl.pallas_call(functools.partial(main_kernel, nx, ny, planes, chans, slab...]
where the time goes in v2:
time: 139 us; the launch traced here: 136 us
  Pallas kernels  135 us (97%)
    pallas_call x1, Pallas kernels, main_pass(): pl.pallas_call(functools.partial(main_kernel, nx, ny, planes, chans, slab...  125 us
    pallas_call x1, Pallas kernels, last_pass(): pl.pallas_call(last_kernel, grid=(planes, parts), out_shape=(shape, jax.S...  10.6 us

profile of v2, /device:TPU:25, one launch (start us, length us, event | category | flops | bytes accessed | tf_op | source)
XLA Modules:
  0.0 136.0 jit_solution(3354840000120894127)
XLA Ops:
  0.6 0.0 copy-start
  0.6 124.8 %main_pass.1 = (bf16[4,64,32,512]{3,2,1,0:T(8,128)(2,1)S(1)}, bf16[4,64,32,512]{3,2,1,0:T(8,128)(2,1)S(1)}, bf16[4,16,128,128]{3,2,1,0:T(8,128)(2,1)S(1)}, bf16[...) custom-call(bf16[4,64,32,512]{3,2,1,0:T(8,128)(2,1)} %flow_hbm.1, bf16[4,64,32,512]{3,2,1,0:T(8,128)(2,1)} %cot_hbm.1, ...), custom_call_target="tpu_custom_call" | custom-call | tf_op jit(solution)/shard_map/main_pass/pallas_call | solution.py:476
  125.4 0.0 copy-done
  125.4 10.6 %last_pass.1 = (bf16[4,64,32,512]{3,2,1,0:T(8,128)(2,1)}, f32[256,64,128]{2,1,0:T(8,128)}, bf16[4,64,32,512]{3,2,1,0:T(8,128)(2,1)}) custom-call(bf16[4,64,32,512]{3,2,1,0:T(8,128)(2,1)S(1)} %get-tuple-element.11.thru_ref, bf16[4,16,128,128]{3,2,1,0:T(8,128)(2,1)S(1)} %get-tuple-element.12.g_ref, bf16[128,512]{1,0:T(8,128)(2,1)S(1)} %copy-done, ...), custom_call_target="tpu_custom_call" | custom-call | tf_op jit(solution)/shard_map/last_pass/pallas_call | solution.py:580
Async XLA Ops:
  0.6 124.8 %copy-start = (bf16[128,512]{1,0:T(8,128)(2,1)S(1)}, bf16[128,512]{1,0:T(8,128)(2,1)}, u32[]{:S(2)}) copy-start(bf16[128,512]{1,0:T(8,128)(2,1)} %constant.13.fy_ref.yt_ref) | copy-start | bytes 393220

commit v3 on v2

--- a/solution.py
+++ b/solution.py
@@ -172,7 +172,7 @@
     def send_sums(f, p):
         @pl.when(at_outer)
         def _():
-            for i, dest in enumerate((inner, far_inner, far_outer)):
+            for i, dest in ((2, far_outer), (1, far_inner), (0, inner)):
                 sums_near(f, p, i, dest, inner).start()
 
         @pl.when(at_inner)
@@ -182,23 +182,19 @@
     def relay_sums(f, p):
         @pl.when(at_inner)
         def _():
-            for i in range(3):
-                sums_near(f, p, i, gy, outer).wait_recv()
-            for i, dest in enumerate((far_inner, far_outer)):
+            for i, dest in ((1, far_outer), (0, far_inner)):
+                sums_near(f, p, 1 + i, gy, outer).wait_recv()
                 zq[f, p, i] = (zr[f, p, 1 + i].astype(f32) + zs[f, p, dest].astype(f32)).astype(bf16)
                 sums_far(f, p, i, dest).start()
 
     def take_sums(f, p):
-        @pl.when(at_outer)
-        def _():
-            sums_near(f, p, 0, gy, inner).wait_recv()
-
+        sums_near(f, p, 0, gy, partner).wait_recv()
         sums_far(f, p, 0, far_inner).wait_recv()
         return zs[f, p, gy].astype(f32) + zr[f, p, 0].astype(f32) + zr[f, p, 3].astype(f32)
 
     def send_mixed(f, p):
+        mixed_near(f, p, 1, gy, far_inner).start()
         mixed_near(f, p, 0, gy, partner).start()
-        mixed_near(f, p, 1, gy, far_inner).start()
 
     def relay_mixed(f, p):
         @pl.when(at_inner)
@@ -334,28 +330,39 @@
         lax.fori_loop(0, groups, turn, 0, unroll=4)
 
     def pieces(lo, hi, p):
-        def piece(s, carry):
+        def place(s):
             h, y = s // parts, s % parts
-            rows16 = pl.ds(pl.multiple_of(h * PACK, PACK), PACK)
-            cols = pl.ds(pl.multiple_of(y * width, width), width)
-            xs[...] = fbuf[p, :, rows16, cols].reshape(chans * PACK, width)
-            r = jnp.dot(kron[...], xs[...], preferred_element_type=f32)
+            return h, pl.ds(h * PACK, PACK), pl.ds(y * width, width)
+
+        def product(s, into):
+            h, rows16, cols = place(s)
+            xs[s % 2] = fbuf[p, :, rows16, cols].reshape(chans * PACK, width)
+            r = jnp.dot(kron[...], xs[s % 2], preferred_element_type=f32)
             r = r + jnp.dot(gt[h], iy_ref[:, cols], preferred_element_type=f32)
-            pre[...] = r.reshape(chans, PACK, width)
-
-            def one(c, inner):
-                v = pre[c] + bias_ref[c]
-                phi = 0.5 + 0.5 * lax.erf(v * root_half)
-                density = jnp.exp(-0.5 * v * v) * density_norm
-                cot = cbuf[p, c, rows16, cols].astype(f32)
-                cbuf[p, c, rows16, cols] = (v * phi).astype(bf16)
-                fbuf[p, c, rows16, cols] = (cot * (phi + v * density)).astype(bf16)
-                return inner
-
-            lax.fori_loop(0, chans, one, 0, unroll=8)
-            return carry
-
-        lax.fori_loop(lo, hi, piece, 0)
+            into[...] = r.reshape(chans, PACK, width)
+
+        def one(s, held, c):
+            _, rows16, cols = place(s)
+            v = held[c] + bias_ref[c]
+            phi = 0.5 + 0.5 * lax.erf(v * root_half)
+            density = jnp.exp(-0.5 * v * v) * density_norm
+            cot = cbuf[p, c, rows16, cols].astype(f32)
+            cbuf[p, c, rows16, cols] = (v * phi).astype(bf16)
+            fbuf[p, c, rows16, cols] = (cot * (phi + v * density)).astype(bf16)
+
+        def rest(s, held):
+            def body(c, carry):
+                one(s, held, c)
+                return carry
+
+            lax.fori_loop(0, chans, body, 0, unroll=8)
+
+        product(lo, pre.at[0])
+        for s in range(lo + 1, hi):
+            product(s, pre.at[s - lo])
+            for c in range(chans):
+                one(s - 1, pre.at[s - 1 - lo], c)
+        rest(hi - 1, pre.at[hi - 1 - lo])
 
     total = halves * parts
 
@@ -373,8 +380,8 @@
             h, y = s // parts, s % parts
             rows16 = pl.ds(pl.multiple_of(h * PACK, PACK), PACK)
             cols = pl.ds(pl.multiple_of(y * width, width), width)
-            xs[...] = fbuf[p, :, rows16, cols].reshape(chans * PACK, width)
-            r = jnp.dot(kron_t[...], xs[...], preferred_element_type=f32)
+            xs[0] = fbuf[p, :, rows16, cols].reshape(chans * PACK, width)
+            r = jnp.dot(kron_t[...], xs[0], preferred_element_type=f32)
             fbuf[p, :, rows16, cols] = r.astype(bf16).reshape(chans, PACK, width)
             return carry
 
@@ -429,10 +436,10 @@
     home = lambda fn: functools.partial(fn, 1)
     half = lambda i: functools.partial(point_part, i)
     plan = (
-        (0, forth(across)),
         (6, home(across)),
         (8, home(relay_mixed)),
         (7, home(mix)),
+        (0, forth(across)),
         (10, through),
         (1, forth(relay_sums)),
         (3, forth(expand)),
@@ -501,8 +508,8 @@
             pltpu.VMEM((2, planes, nx, groups, jg, LANES), bf16),
             pltpu.VMEM((planes, groups, modes, LANES), bf16),
             pltpu.VMEM((slab // PACK, tall, modes), bf16),
-            pltpu.VMEM((chans, PACK, 2 * LANES), f32),
-            pltpu.VMEM((tall, 2 * LANES), bf16),
+            pltpu.VMEM((2, chans, PACK, 2 * LANES), f32),
+            pltpu.VMEM((2, tall, 2 * LANES), bf16),
             dma((planes,)), dma((planes,)), dma,
             dma((2, planes, nx)), dma((2, planes, nx)),
             dma((2, planes, ny)), dma((2, planes, ny)),

time: 139 us -> 133 us (0.957)
  Pallas kernels: 135 us -> 130 us
    pallas_call x1, Pallas kernels: 125 us -> 119 us  [main_pass(): pl.pallas_call(functools.partial(main_kernel, nx, ny, planes, chans, slab...]
where the time goes in v3:
time: 133 us; the launch traced here: 130 us
  Pallas kernels  130 us (98%)
    pallas_call x1, Pallas kernels, main_pass(): pl.pallas_call(functools.partial(main_kernel, nx, ny, planes, chans, slab...  119 us
    pallas_call x1, Pallas kernels, last_pass(): pl.pallas_call(last_kernel, grid=(planes, parts), out_shape=(shape, jax.S...  10.6 us

profile of v3, /device:TPU:25, one launch (start us, length us, event | category | flops | bytes accessed | tf_op | source)
XLA Modules:
  0.0 130.4 jit_solution(17380901722334783894)
XLA Ops:
  0.6 0.0 copy-start
  0.6 119.2 %main_pass.1 = (bf16[4,64,32,512]{3,2,1,0:T(8,128)(2,1)S(1)}, bf16[4,64,32,512]{3,2,1,0:T(8,128)(2,1)S(1)}, bf16[4,16,128,128]{3,2,1,0:T(8,128)(2,1)S(1)}, bf16[...) custom-call(bf16[4,64,32,512]{3,2,1,0:T(8,128)(2,1)} %flow_hbm.1, bf16[4,64,32,512]{3,2,1,0:T(8,128)(2,1)} %cot_hbm.1, ...), custom_call_target="tpu_custom_call" | custom-call | tf_op jit(solution)/shard_map/main_pass/pallas_call | solution.py:483
  119.9 0.0 copy-done
  119.9 10.6 %last_pass.1 = (bf16[4,64,32,512]{3,2,1,0:T(8,128)(2,1)}, f32[256,64,128]{2,1,0:T(8,128)}, bf16[4,64,32,512]{3,2,1,0:T(8,128)(2,1)}) custom-call(bf16[4,64,32,512]{3,2,1,0:T(8,128)(2,1)S(1)} %get-tuple-element.11.thru_ref, bf16[4,16,128,128]{3,2,1,0:T(8,128)(2,1)S(1)} %get-tuple-element.12.g_ref, bf16[128,512]{1,0:T(8,128)(2,1)S(1)} %copy-done, ...), custom_call_target="tpu_custom_call" | custom-call | tf_op jit(solution)/shard_map/last_pass/pallas_call | solution.py:587
Async XLA Ops:
  0.6 119.2 %copy-start = (bf16[128,512]{1,0:T(8,128)(2,1)S(1)}, bf16[128,512]{1,0:T(8,128)(2,1)}, u32[]{:S(2)}) copy-start(bf16[128,512]{1,0:T(8,128)(2,1)} %constant.13.fy_ref.yt_ref) | copy-start | bytes 393220
